TPU v7x, 128 devices: a whole 4x4x4 slice. The times are simulated.
128 devices in a mesh: var: 32 (over y, z, core), samp: 4 (over x).
Axes of the slice: x: 4, y: 4, z: 4, core: 2. Of those that a mesh axis runs over, the one named last changes fastest.
Arguments:
- genotypes: bfloat16 [49152, 16384], P('samp', 'var'), may hold values from -4 to 4
- labels: int32 [49152, 256], P(('samp', 'var')), may hold values 0 or 1
- act_coef: bfloat16 [16, 8192], P(None, 'var'), may hold values from -0.125 to 0.125
- act_index: int32 [8192], P('var'), may hold values from 0 to 511, as said below
- act_count: int32 [32], P('var'), may hold values from 1 to 256, as said below
- loadings: float32 [16, 256], replicated, may hold values from -1.5 to 1.5
- intercept: float32 [256], replicated, may hold values from -2.5 to 0.5
Outputs:
- grad_var: float32 [16, 16384], P(None, 'var')
- grad_trait: float32 [16, 256], replicated
- inactive_score: float32 [16384], P('var')
- top_score: float32 [1], replicated
Inputs may be any that keep to these rules, and one draw needn't show every extreme that they name: `act_index`: within each aligned block of 256 slots (one index of var) the numbers are distinct; slots past that block's count are padding and carry no variant. `act_count`: some index of var has all 256 slots live.
All inputs are finite; a program needn't handle non-finite values. No bound on the sum of `labels` on one device may be relied on, other than what follows from the above.
Results may differ from a plain program's by a relative error of at most 0.0033.
Values may be sent and summed in bfloat16 or wider, within the bound.
A program may use at most 64 MiB of HBM per device.

v0:
```python
import math

import jax
import jax.numpy as jnp
from jax import lax
from jax.sharding import PartitionSpec as P


def in_blocks(shard, dim, peers):
    dims = shard.shape
    parts = shard.reshape(*dims[:dim], peers, dims[dim] // peers, *dims[dim + 1 :])
    return jnp.moveaxis(parts, dim, 0)


def summed_on_arrival(shard, axis, dim):
    peers = lax.axis_size(axis)
    parts = lax.all_to_all(in_blocks(shard, dim, peers), axis, 0, 0, tiled=True)
    return jnp.sum(parts.astype(jnp.float32), axis=0)


def over_pieces(shard, axis):
    parts = lax.all_gather(shard, axis)
    return parts.sum(axis=0)


def laid_out(parts, dim):
    parts = jnp.moveaxis(parts, 0, dim)
    dims = parts.shape
    return parts.reshape(*dims[:dim], dims[dim] * dims[dim + 1], *dims[dim + 2 :])


def from_everyone(shard, axis):
    peers = lax.axis_size(axis)
    return lax.all_to_all(
        jnp.broadcast_to(shard[None], (peers, *shard.shape)), axis, 0, 0, tiled=True
    )


def gathered_copies(shard, axis, dim):
    return laid_out(from_everyone(shard, axis), dim)


def taken_together(shard, axis):
    return from_everyone(shard, axis).sum(axis=0)


def of_everyone(shard, axis):
    return from_everyone(shard, axis).max(axis=0)


def per_device(genotypes, labels, act_coef, act_index, act_count, loadings, intercept):
    sample_rows = genotypes.shape[0]
    width = genotypes.shape[1]
    norm = 1.0 / math.sqrt(sample_rows * lax.axis_size("samp"))
    live = jnp.arange(act_index.shape[0], dtype=jnp.int32) < act_count[0]
    chosen = (act_index[:, None] == jnp.arange(width, dtype=jnp.int32)[None, :]) & live[:, None]
    active = jnp.any(chosen, axis=0)
    dense = jnp.dot(
        act_coef, chosen.astype(jnp.bfloat16), preferred_element_type=jnp.float32
    ).astype(jnp.bfloat16)
    predictor = lax.dot_general(
        dense, genotypes, (((1,), (1,)), ((), ())), preferred_element_type=jnp.float32
    )
    mine = summed_on_arrival(predictor.astype(jnp.bfloat16), "var", 1)
    eta = (
        jnp.einsum("rs,rt->st", mine, loadings, precision=lax.Precision.HIGHEST)
        + intercept[None, :]
    )
    resid = jax.nn.sigmoid(eta) - labels.astype(jnp.float32)
    weights = jnp.einsum("rt,st->rs", loadings, resid, precision=lax.Precision.HIGHEST).astype(
        jnp.bfloat16
    )
    trait_part = jnp.einsum("rs,st->rt", mine, resid, precision=lax.Precision.HIGHEST) * norm
    grad_trait = over_pieces(trait_part, ("var", "samp"))
    variant_part = jnp.dot(
        gathered_copies(weights, "var", 1), genotypes, preferred_element_type=jnp.float32
    )
    grad_var = taken_together(variant_part * norm, "samp")
    score = jnp.sqrt(jnp.sum(grad_var * grad_var, axis=0))
    inactive_score = jnp.where(active, jnp.float32(0.0), score)
    local_top = jnp.max(inactive_score)
    top_value = of_everyone(local_top, "var")
    return (grad_var, grad_trait, inactive_score, jnp.reshape(top_value, (1,)))


def solution(mesh):
    placed = (
        P("samp", "var"),
        P(("samp", "var"), None),
        P(None, "var"),
        P("var"),
        P("var"),
        P(),
        P(),
    )
    return jax.shard_map(
        per_device,
        mesh=mesh,
        in_specs=placed,
        out_specs=(P(None, "var"), P(), P("var"), P()),
        check_vma=False,
    )
```

profile of v0, /device:TPU:1, one launch (start us, length us, event | category | flops | bytes accessed | tf_op | source)
XLA Modules:
  0.0 109.9 jit_solution(9361733463114576242)
XLA Ops:
  7.2 0.0 copy-start
  7.2 0.0 all-gather.3.cloned.1.call-start
  7.9 8.2 %convolution_convert_fusion = bf16[16,12288]{1,0:T(8,128)(2,1)S(1)} fusion(bf16[12288,512]{1,0:T(8,128)(2,1)} %param.7, bf16[16,256]{1,0:T(8,128)(2,1)} %param.9, s32[256]{0:T(256)} %param.10, pred[256]{0:T(512)(128)(4,1)S(1)} %iota_compare_fusion.1), kind=kOutput, calls=%fused_computation | convolution fusion | flops 205987840 | bytes 12985600 | tf_op jit(solution)/shard_map/dot_general | solution.py:61
  16.1 0.1 copy.22
  16.2 19.7 %all_to_all.21 = bf16[32,16,384]{2,1,0:T(8,128)(2,1)S(1)} all-to-all(bf16[32,16,384]{2,1,0:T(8,128)(2,1)S(1)} %bitcast.29), channel_id=1, replica_groups=mesh['var'=32,'samp'=4] {'var'}, dimensions={0} | all-to-all | bytes 786432 | tf_op jit(solution)/shard_map/all_to_all | solution.py:17
  35.9 0.1 convert_reduce_fusion
  36.0 0.6 fusion.4
  36.6 0.9 convolution_multiply_fusion.1
  37.5 0.0 all-gather.3.cloned.1.call-update
  37.5 0.4 fusion.5
  37.9 0.1 broadcast_in_dim.9
  38.0 13.6 %all_to_all.22 = bf16[32,16,384]{2,1,0:T(8,128)(2,1)S(1)} all-to-all(bf16[32,16,384]{2,1,0:T(8,128)(2,1)S(1)} %broadcast_in_dim.9), channel_id=1, replica_groups=mesh['var'=32,'samp'=4] {'var'}, dimensions={0} | all-to-all | bytes 786432 | tf_op jit(solution)/shard_map/all_to_all | solution.py:34
  51.7 6.3 %convolution_multiply_fusion = f32[16,512]{1,0:T(8,128)S(1)} fusion(bf16[16,12288]{1,0:T(8,128)(2,1)S(1)} %bitcast.26, bf16[12288,512]{1,0:T(8,128)(2,1)} %param.7), kind=kOutput, calls=%fused_computation.7 | convolution fusion | flops 201334784 | bytes 13008896 | tf_op jit(solution)/shard_map/dot_general | solution.py:75
  58.0 0.7 broadcast_in_dim.10
  58.7 4.0 %all-to-all-start.2 = ((f32[4,16,512]{2,1,0:T(8,128)}), f32[4,16,512]{2,1,0:T(8,128)S(1)}, u32[]{:S(2)}, u32[]{:S(2)}) async-start(f32[4,16,512]{2,1,0:T(8,128)} %broadcast_in_dim.10), calls=%async_computation.2 | async-start | bytes 262144 | tf_op jit(solution)/shard_map/all_to_all | solution.py:34
  62.7 0.1 fusion.7
  62.8 4.7 %all-to-all-done.2 = f32[4,16,512]{2,1,0:T(8,128)S(1)} async-done(((f32[4,16,512]{2,1,0:T(8,128)}), f32[4,16,512]{2,1,0:T(8,128)S(1)}, u32[]{:S(2)}, u32[]{:S(2)}) %all-to-all-start.2) | async-done | bytes 131104 | tf_op jit(solution)/shard_map/all_to_all | solution.py:34
  67.6 0.0 copy-start.1
  67.6 1.2 %fusion.14 = (f32[]{:T(128)}, f32[512]{0:T(512)}) fusion(pred[512]{0:T(512)(128)(4,1)S(1)} %fusion.7, f32[512]{0:T(512)S(1)} %multiply_reduce_fusion), kind=kLoop, calls=%fused_computation.22 | loop fusion | flops 1023 | bytes 4612 | tf_op jit(solution)/shard_map/reduce_max | solution.py:81
  68.8 0.7 broadcast_in_dim.12
  69.4 11.7 %all_to_all.23 = f32[32,1,1]{2,1,0:T(1,128)S(1)} all-to-all(f32[32,1,1]{2,1,0:T(1,128)S(1)} %broadcast_in_dim.12), channel_id=1, replica_groups=mesh['var'=32,'samp'=4] {'var'}, dimensions={0} | all-to-all | bytes 256 | tf_op jit(solution)/shard_map/all_to_all | solution.py:34
  81.1 0.6 reduce_max.19
  81.8 18.9 %all-gather.3.cloned.1.call-done = f32[2048,256]{1,0:T(8,128)} async-done(((f32[16,256]{1,0:T(8,128)}), f32[2048,256]{1,0:T(8,128)}) %all-gather.3.cloned.1.call-update) | async-done | bytes 2097168 | tf_op jit(solution)/shard_map/all_gather | solution.py:22
  100.7 2.4 %reduce_sum.38 = f32[16,256]{1,0:T(8,128)} reduce(f32[128,16,256]{2,1,0:T(8,128)} %bitcast.27, f32[]{:T(128)} %constant.0.clone.1), dimensions={0}, to_apply=%region_2.0 | reduce | flops 520192 | bytes 2113540 | tf_op jit(solution)/shard_map/reduce_sum | solution.py:23
  (12 shorter events, 0.1 us)
Async XLA Ops:
  7.2 28.8 %copy-start = (f32[16,256]{1,0:T(8,128)S(1)}, f32[16,256]{1,0:T(8,128)}, u32[]{:S(2)}) copy-start(f32[16,256]{1,0:T(8,128)} %param.12) | copy-start | bytes 49156
  7.2 28.8 %copy-start.4 = (f32[256]{0:T(256)S(1)}, f32[256]{0:T(256)}, u32[]{:S(2)}) copy-start(f32[256]{0:T(256)} %param.13) | copy-start | bytes 3076
  7.2 28.8 %copy-start.3 = (s32[384,256]{1,0:T(8,128)S(1)}, s32[384,256]{1,0:T(8,128)}, u32[]{:S(2)}) copy-start(s32[384,256]{1,0:T(8,128)} %param.8) | copy-start | bytes 1179652
  7.2 93.4 %all-gather.3.cloned.1.call-start = ((), (), s32[]{:S(2)}) async-start(), calls=%async_computation.4 | async-start | bytes 2113536 | tf_op jit(solution)/shard_map/all_gather | solution.py:22
  36.5 26.1 %copy-start.2 = (s32[256]{0:T(256)S(1)}, s32[256]{0:T(256)}, u32[]{:S(2)}) copy-start(s32[256]{0:T(256)} %param.10) | copy-start | bytes 3076
  58.7 8.9 %all-to-all-start.2 = ((f32[4,16,512]{2,1,0:T(8,128)}), f32[4,16,512]{2,1,0:T(8,128)S(1)}, u32[]{:S(2)}, u32[]{:S(2)}) async-start(f32[4,16,512]{2,1,0:T(8,128)} %broadcast_in_dim.10), calls=%async_computation.2 | async-start | bytes 262144 | tf_op jit(solution)/shard_map/all_to_all | solution.py:34
  67.6 35.5 %copy-start.1 = (f32[16,512]{1,0:T(8,128)}, f32[16,512]{1,0:T(8,128)S(1)}, u32[]{:S(2)}) copy-start(f32[16,512]{1,0:T(8,128)S(1)} %reduce_sum.37) | copy-start | bytes 98308
Sparse Core Ops, SparseCore 0:
  37.6 62.9 all-gather.2
where the time goes:
time: 110 us
  blocking collectives  45 us (41%)
  waiting for transfers between devices  23.6 us (21%)
  matrix products  16.4 us (15%)
  between operations  14.8 us (13%)
  other arithmetic  4.46 us (4%)
  starting transfers between devices  4.05 us (4%)
  local copies, waits for them, and re-layouts  1.53 us (1%)
    all_to_all x2, blocking collectives, from_everyone(): lax.all_to_all(jnp.broadcast_to(shard[None], (peers, *shard.shape)), axis...  25.3 us
    all_to_all x1, blocking collectives, summed_on_arrival(): parts = lax.all_to_all(in_blocks(shard, dim, peers), axis, 0, 0, tiled=True)  19.7 us
    all_gather x1, waiting for transfers between devices, over_pieces(): parts = lax.all_gather(shard, axis)  18.9 us
    dot_general x1, matrix products, per_device(): lax.dot_general(dense, genotypes, (((1,), (1,)), ((), ())), preferred_ele...  8.19 us
    dot_general x1, matrix products, per_device(): jnp.dot(gathered_copies(weights, 'var', 1), genotypes, preferred_element_...  6.3 us
    all_to_all x1, waiting for transfers between devices, from_everyone(): lax.all_to_all(jnp.broadcast_to(shard[None], (peers, *shard.shape)), axis...  4.71 us
    all_to_all x1, starting transfers between devices, from_everyone(): lax.all_to_all(jnp.broadcast_to(shard[None], (peers, *shard.shape)), axis...  4.01 us
    reduce_sum x1, other arithmetic, over_pieces(): return parts.sum(axis=0)  2.38 us
  transfers between devices with their start and end apart: 2, of which 2 were waited for; matrix products, arithmetic and copies ran while one was open for 9% of the time, Pallas kernels for 0%

commit v1 on v0

v1 whole, which is shorter than its diff:
```python
import functools
import math

import jax
import jax.numpy as jnp
from jax import lax
from jax.experimental import pallas as pl
from jax.experimental.pallas import tpu as pltpu
from jax.sharding import PartitionSpec as P

MESH = pl.DeviceIdType.MESH
F32 = jnp.float32
BF16 = jnp.bfloat16
SIDE = 4
CHIPS = SIDE * SIDE
XS = 4
NT = (((1,), (1,)), ((), ()))
TN = (((0,), (0,)), ((), ()))
NN = (((1,), (0,)), ((), ()))


def div(a, b):
    return lax.div(a, jnp.int32(b))


def rem(a, b):
    return lax.rem(a, jnp.int32(b))


def stride(i):
    return rem(10 - div(i * (i + 1), 2), SIDE)


def dot(a, b, dims):
    return lax.dot_general(a, b, dims, preferred_element_type=F32)


def halves(x):
    high = x.astype(BF16)
    return high, (x - high.astype(F32)).astype(BF16)


def kernel(
    norm, geno_hbm, labels_hbm, coef_hbm, index_hbm, count_hbm, load_hbm, icpt_hbm,
    gv_ref, gt_ref, score_ref, top_ref,
    geno, labels, coef, index, count, load, icpt,
    pair_out, pair_in, pred_out, pred_in, w_same, w_pair, vp, tops,
    tr_own, tr_core, tr_x, tr_y, tr_z,
    geno_sem, small_sem, pair_send, pair_recv, pred_send, pred_recv,
    w_send, w_recv, relay_send, relay_recv, vp_send, vp_recv, top_send, top_recv,
    tr_send, tr_core_recv, tr_x_recv, tr_y_recv, tr_z_recv,
):
    me = lax.axis_index("var")
    samp = lax.axis_index("samp")
    core = rem(me, 2)
    chip = div(me, 2)
    y, z = div(chip, SIDE), rem(chip, SIDE)
    other = 1 - core
    partner = chip * 2 + other

    def to_chip(i):
        return rem(y + stride(div(i, SIDE)), SIDE) * SIDE + rem(z + stride(rem(i, SIDE)), SIDE)

    def from_chip(i):
        return rem(y + SIDE - stride(div(i, SIDE)), SIDE) * SIDE + rem(
            z + SIDE - stride(rem(i, SIDE)), SIDE
        )

    def send(src, dst, send_sem, recv_sem, var, samp_at):
        return pltpu.make_async_remote_copy(
            src_ref=src,
            dst_ref=dst,
            send_sem=send_sem,
            recv_sem=recv_sem,
            device_id=(var, samp_at),
            device_id_type=MESH,
        )

    small = [
        pltpu.make_async_copy(src, dst, small_sem.at[k])
        for k, (src, dst) in enumerate(
            (
                (index_hbm, index),
                (count_hbm, count),
                (coef_hbm, coef),
                (load_hbm, load),
                (icpt_hbm, icpt),
                (labels_hbm, labels),
            )
        )
    ]
    for copy in small[:5]:
        copy.start()
    rows = labels.shape[0]

    def geno_copy(i, which):
        at = to_chip(i) * 2 + which
        return pltpu.make_async_copy(
            geno_hbm.at[pl.ds(pl.multiple_of(at * rows, rows), rows)], geno.at[at], geno_sem.at[at]
        )

    def start_geno(i, carry, which):
        geno_copy(i, which).start()
        return carry

    lax.fori_loop(0, CHIPS, functools.partial(start_geno, which=other), 0)
    lax.fori_loop(0, CHIPS, functools.partial(start_geno, which=core), 0)
    small[5].start()

    barrier = pltpu.get_barrier_semaphore()

    def greet(i, carry):
        for which in range(2):
            pl.semaphore_signal(
                barrier, inc=1, device_id=(to_chip(i) * 2 + which, samp), device_id_type=MESH
            )
        return carry

    lax.fori_loop(0, CHIPS - 1, greet, 0)
    pl.semaphore_signal(barrier, inc=1, device_id=(partner, samp), device_id_type=MESH)
    for step in range(1, XS):
        pl.semaphore_signal(
            barrier, inc=1, device_id=(me, rem(samp + step, XS)), device_id_type=MESH
        )

    for copy in small[:5]:
        copy.wait()
    slots = index.shape[1]
    width = geno.shape[2]
    lane = lax.broadcasted_iota(jnp.int32, (1, slots), 1)
    live = lane < count[...]
    variant = lax.broadcasted_iota(jnp.int32, (width, slots), 0)
    chosen = jnp.where((variant == index[...]) & live, F32(1.0), F32(0.0)).astype(BF16)
    dense = dot(coef[...], chosen, NT).astype(BF16)
    active = dot(jnp.where(live, F32(1.0), F32(0.0)).astype(BF16), chosen, NT)

    def for_partner(k, carry):
        for u in range(2):
            i = k * 2 + u
            geno_copy(i, other).wait()
        for u in range(2):
            i = k * 2 + u
            part = dot(dense, geno[to_chip(i) * 2 + other], NT)
            pair_out[i] = part.astype(BF16)
        return carry

    lax.fori_loop(0, CHIPS // 2, for_partner, 0)

    pl.semaphore_wait(barrier, 2 * CHIPS - 1 + XS - 1)
    to_pair = send(pair_out, pair_in, pair_send, pair_recv, partner, samp)
    to_pair.start()

    def pred_copy(i):
        return send(
            pred_out.at[i],
            pred_in.at[i],
            pred_send.at[i],
            pred_recv.at[i],
            to_chip(i) * 2 + core,
            samp,
        )

    to_pair.wait_recv()

    def for_same(k, carry):
        for u in range(2):
            i = k * 2 + u
            geno_copy(i, core).wait()
        for u in range(2):
            i = k * 2 + u
            part = dot(dense, geno[to_chip(i) * 2 + core], NT)
            pred_out[i] = (part + pair_in[i].astype(F32)).astype(BF16)
            pred_copy(i).start()
        return carry

    lax.fori_loop(0, CHIPS // 2 - 1, for_same, 0)
    last = CHIPS - 2
    geno_copy(last, core).wait()
    part = dot(dense, geno[to_chip(last) * 2 + core], NT)
    pred_out[last] = (part + pair_in[last].astype(F32)).astype(BF16)
    pred_copy(last).start()
    geno_copy(CHIPS - 1, core).wait()
    mine = dot(dense, geno[me], NT) + pair_in[CHIPS - 1].astype(F32)

    small[5].wait()
    load_h, load_m = halves(load[...])
    load_both = jnp.concatenate([load_h, load_m], axis=0)

    def add_pred(k, total):
        i = CHIPS - 2 - k
        pred_copy(i).wait_recv()
        return total + pred_in[i].astype(F32)

    mine = lax.fori_loop(0, CHIPS - 1, add_pred, mine)
    mine_h, mine_m = halves(mine)
    eta = (
        dot(
            jnp.concatenate([mine_h, mine_h, mine_m], axis=0),
            jnp.concatenate([load_h, load_m, load_h], axis=0),
            TN,
        )
        + icpt[...]
    )
    resid = 1.0 / (1.0 + jnp.exp(-eta)) - labels[...].astype(F32)
    resid_h, resid_m = halves(resid)
    first = dot(load_both, resid_h, NT)
    rank = load.shape[0]
    weights = first[:rank] + first[rank:] + dot(load_h, resid_m, NT)
    w_same[CHIPS - 1] = weights.astype(BF16)

    def w_copy(i):
        return send(
            w_same.at[CHIPS - 1],
            w_same.at[i],
            w_send.at[i],
            w_recv.at[i],
            to_chip(i) * 2 + core,
            samp,
        )

    def relay_copy(i):
        return send(
            w_same.at[i], w_pair.at[i], relay_send.at[i], relay_recv.at[i], partner, samp
        )

    def start_w(i, carry):
        w_copy(i).start()
        return carry

    lax.fori_loop(0, CHIPS - 1, start_w, 0)
    relay_copy(CHIPS - 1).start()

    both = dot(jnp.concatenate([mine_h, mine_m], axis=0), resid_h, NN)
    tr_own[...] = (both[:rank] + both[rank:] + dot(mine_h, resid_m, NN)) * norm
    tr_core_copy = send(tr_own, tr_core, tr_send.at[0], tr_core_recv, partner, samp)
    tr_core_copy.start()

    def same_block(i, total):
        w_copy(i).wait_recv()
        relay_copy(i).start()
        return total + dot(w_same[i], geno[from_chip(i) * 2 + core], NN)

    def pair_block(i, total):
        relay_copy(i).wait_recv()
        return total + dot(w_pair[i], geno[from_chip(i) * 2 + other], NN)

    def ring_copies(slots, at, send_base, recv_sems, where):
        return [
            send(
                slots.at[at],
                slots.at[at],
                tr_send.at[send_base + step - 1],
                recv_sems.at[at],
                *where(step),
            )
            for step in range(1, SIDE)
        ]

    def ring_start(value, slots, at, send_base, recv_sems, where):
        slots[at] = value
        copies = ring_copies(slots, at, send_base, recv_sems, where)
        for copy in copies:
            copy.start()
        return copies

    def ring_sum(slots, at, recv_sems, where):
        for step in range(1, SIDE):
            source = rem(at + step, SIDE)
            send(
                slots.at[source], slots.at[source], tr_send.at[0], recv_sems.at[source], *where(1)
            ).wait_recv()
        return (slots[0] + slots[1]) + (slots[2] + slots[3])

    def along_x(step):
        return me, rem(samp + step, XS)

    def along_y(step):
        return (rem(y + step, SIDE) * SIDE + z) * 2 + core, samp

    def along_z(step):
        return (y * SIDE + rem(z + step, SIDE)) * 2 + core, samp

    def blocks(low, high, total):
        def block(k, total):
            i = high - 1 - k
            total = same_block(i, total)
            return pair_block(i + 1, total)

        return lax.fori_loop(0, high - low, block, total)

    total = dot(w_same[CHIPS - 1], geno[me], NN)
    total = blocks(11, 15, total)
    tr_core_copy.wait_recv()
    x_copies = ring_start(tr_own[...] + tr_core[...], tr_x, samp, 1, tr_x_recv, along_x)
    total = blocks(5, 11, total)
    x_total = ring_sum(tr_x, samp, tr_x_recv, along_x)
    y_copies = ring_start(x_total, tr_y, y, 4, tr_y_recv, along_y)
    total = blocks(0, 5, total)
    total = pair_block(0, total)

    vp[samp] = total.astype(BF16)

    def vp_copy(step):
        return send(
            vp.at[samp],
            vp.at[samp],
            vp_send.at[step - 1],
            vp_recv.at[samp],
            me,
            rem(samp + step, XS),
        )

    for step in range(1, XS):
        vp_copy(step).start()
    y_total = ring_sum(tr_y, y, tr_y_recv, along_y)
    z_copies = ring_start(y_total, tr_z, z, 7, tr_z_recv, along_z)
    for step in range(1, XS):
        source = rem(samp + step, XS)
        send(
            vp.at[source], vp.at[source], vp_send.at[0], vp_recv.at[source], me, rem(samp + 1, XS)
        ).wait_recv()
    grad = vp[0].astype(F32)
    for source in range(1, XS):
        grad = grad + vp[source].astype(F32)
    grad = grad * norm
    gv_ref[...] = grad
    score = jnp.sqrt(jnp.sum(grad * grad, axis=0, keepdims=True))
    score = jnp.where(active > 0.0, F32(0.0), score)
    score_ref[...] = score
    best = score[:, :128]
    for at in range(128, width, 128):
        best = jnp.maximum(best, score[:, at : at + 128])
    tops[2 * CHIPS - 2] = best

    def top_copy(i, which):
        slot = i * 2 + which
        target = to_chip(i) * 2 + (core if which == 0 else other)
        return send(
            tops.at[2 * CHIPS - 2],
            tops.at[slot],
            top_send.at[slot],
            top_recv.at[slot],
            target,
            samp,
        )

    def start_top(i, carry):
        top_copy(i, 0).start()
        top_copy(i, 1).start()
        return carry

    lax.fori_loop(0, CHIPS - 1, start_top, 0)
    top_copy(CHIPS - 1, 1).start()

    z_total = ring_sum(tr_z, z, tr_z_recv, along_z)
    gt_ref[...] = z_total

    to_pair.wait_send()

    def sent(i, carry):
        pred_copy(i).wait_send()
        w_copy(i).wait_send()
        relay_copy(i).wait_send()
        return carry

    lax.fori_loop(0, CHIPS - 1, sent, 0)
    relay_copy(CHIPS - 1).wait_send()
    tr_core_copy.wait_send()
    for copy in (*x_copies, *y_copies, *z_copies):
        copy.wait_send()
    for step in range(1, XS):
        vp_copy(step).wait_send()

    def top_wait(i, carry):
        for which in range(2):
            top_copy(i, which).wait()
        return carry

    lax.fori_loop(0, CHIPS - 1, top_wait, 0)
    top_copy(CHIPS - 1, 1).wait()
    top = jnp.max(tops[...], axis=0)
    top_ref[...] = jnp.max(top, axis=1, keepdims=True)


def per_device(genotypes, labels, act_coef, act_index, act_count, loadings, intercept):
    sample_rows, width = genotypes.shape
    rows, traits = labels.shape
    rank = loadings.shape[0]
    slots = act_index.shape[0]
    norm = 1.0 / math.sqrt(sample_rows * lax.axis_size("samp"))
    dma = pltpu.SemaphoreType.DMA
    hbm = pl.BlockSpec(memory_space=pl.ANY)
    vmem = pl.BlockSpec(memory_space=pltpu.VMEM)
    blocks = (CHIPS, rank, rows)
    trait = (rank, traits)
    grad_var, grad_trait, score, top = pl.pallas_call(
        functools.partial(kernel, norm),
        out_shape=(
            jax.ShapeDtypeStruct((rank, width), F32),
            jax.ShapeDtypeStruct(trait, F32),
            jax.ShapeDtypeStruct((1, width), F32),
            jax.ShapeDtypeStruct((1, 1), F32),
        ),
        in_specs=[hbm] * 7,
        out_specs=(vmem,) * 4,
        scratch_shapes=[
            pltpu.VMEM((2 * CHIPS, rows, width), BF16),
            pltpu.VMEM((rows, traits), jnp.int32),
            pltpu.VMEM((rank, slots), BF16),
            pltpu.VMEM((1, slots), jnp.int32),
            pltpu.VMEM((1, 1), jnp.int32),
            pltpu.VMEM(trait, F32),
            pltpu.VMEM((1, traits), F32),
            pltpu.VMEM(blocks, BF16),
            pltpu.VMEM(blocks, BF16),
            pltpu.VMEM(blocks, BF16),
            pltpu.VMEM(blocks, BF16),
            pltpu.VMEM(blocks, BF16),
            pltpu.VMEM(blocks, BF16),
            pltpu.VMEM((XS, rank, width), BF16),
            pltpu.VMEM((2 * CHIPS, 1, 128), F32),
            pltpu.VMEM(trait, F32),
            pltpu.VMEM(trait, F32),
            pltpu.VMEM((XS, *trait), F32),
            pltpu.VMEM((SIDE, *trait), F32),
            pltpu.VMEM((SIDE, *trait), F32),
            dma((2 * CHIPS,)),
            dma((6,)),
            dma,
            dma,
            dma((CHIPS,)),
            dma((CHIPS,)),
            dma((CHIPS,)),
            dma((CHIPS,)),
            dma((CHIPS,)),
            dma((CHIPS,)),
            dma((XS,)),
            dma((XS,)),
            dma((2 * CHIPS,)),
            dma((2 * CHIPS,)),
            dma((10,)),
            dma,
            dma((XS,)),
            dma((SIDE,)),
            dma((SIDE,)),
        ],
        compiler_params=pltpu.CompilerParams(collective_id=0, has_side_effects=True),
    )(
        genotypes,
        labels,
        act_coef,
        act_index.reshape(1, slots),
        act_count.reshape(1, 1),
        loadings,
        intercept.reshape(1, traits),
    )
    return grad_var, grad_trait, score.reshape(width), top.reshape(1)


def solution(mesh):
    placed = (
        P("samp", "var"),
        P(("samp", "var"), None),
        P(None, "var"),
        P("var"),
        P("var"),
        P(),
        P(),
    )
    return jax.shard_map(
        per_device,
        mesh=mesh,
        in_specs=placed,
        out_specs=(P(None, "var"), P(), P("var"), P()),
        check_vma=False,
    )
```

time: 110 us -> 49.7 us (0.45)
  blocking collectives: 45 us -> 0 us
  Pallas kernels: 0 us -> 42.5 us
  waiting for transfers between devices: 23.6 us -> 0 us
  matrix products: 16.4 us -> 0 us
  between operations: 14.8 us -> 3.04 us
  other arithmetic: 4.46 us -> 0 us
  starting transfers between devices: 4.05 us -> 0 us
  local copies, waits for them, and re-layouts: 1.53 us -> 3.93 us
    all_to_all x3 -> x0, blocking collectives: 45 us -> none  [the longest x2 25.3 us: from_everyone(): lax.all_to_all(jnp.broadcast_to(shard[None], (peers, *shard.shape)), axis...]
    pallas_call x0 -> x1, Pallas kernels: none -> 42.5 us  [per_device(): pl.pallas_call(functools.partial(kernel, norm), out_shape=(jax.ShapeDtype...]
    all_gather x1 -> x0, waiting for transfers between devices: 18.9 us -> none  [over_pieces(): parts = lax.all_gather(shard, axis)]
    dot_general x5 -> x0, matrix products: 16.4 us -> none  [the longest x1 8.19 us: per_device(): lax.dot_general(dense, genotypes, (((1,), (1,)), ((), ())), preferred_ele...]
    all_to_all x1 -> x0, waiting for transfers between devices: 4.71 us -> none  [from_everyone(): lax.all_to_all(jnp.broadcast_to(shard[None], (peers, *shard.shape)), axis...]
    all_to_all x1 -> x0, starting transfers between devices: 4.01 us -> none  [from_everyone(): lax.all_to_all(jnp.broadcast_to(shard[None], (peers, *shard.shape)), axis...]
    unnamed x10 -> x3, local copies, waits for them, and re-layouts: 0.03 us -> 3.93 us
    reduce_sum x4 -> x0, other arithmetic: 2.48 us -> none  [the longest x1 2.38 us: over_pieces(): return parts.sum(axis=0)]
  transfers between devices with their start and end apart: 2 -> 0, of which waited for: 2 -> 0; matrix products, arithmetic and copies ran while one was open for 9% -> 0% of each run, Pallas kernels for 0% -> 0%
where the time goes in v1:
time: 49.7 us; the launch traced here: 49.4 us
  Pallas kernels  42.5 us (86%)
  local copies, waits for them, and re-layouts  3.93 us (8%)
  between operations  3.04 us (6%)
    pallas_call x1, Pallas kernels, per_device(): pl.pallas_call(functools.partial(kernel, norm), out_shape=(jax.ShapeDtype...  42.5 us
    unnamed x3, local copies, waits for them, and re-layouts  3.93 us

profile of v1, /device:TPU:1, one launch (start us, length us, event | category | flops | bytes accessed | tf_op | source)
XLA Modules:
  0.0 49.4 jit_solution(5321976236571022600)
XLA Ops:
  1.3 42.5 %shard_map.102 = (f32[16,512]{1,0:T(8,128)}, f32[16,256]{1,0:T(8,128)}, f32[1,512]{1,0:T(1,128)}, f32[1,1]{1,0:T(1,128)}) custom-call(bf16[12288,512]{1,0:T(8,128)(2,1)} %geno_hbm.1, s32[384,256]{1,0:T(8,128)} %labels_hbm.1, bf16[16,256]{1,0:T(8,128)(2,1)} %coef_hbm.1, s32[1,256]{1,0:T(1,128)} %bitcast.7, s32[1,1]{1,0:T(1,128)} %bitcast.5.count_hbm, ...), custom_call_target="tpu_custom_call" | custom-call | tf_op jit(solution)/shard_map/pallas_call | solution.py:396
  43.8 1.4 %copy.16 = f32[16,512]{1,0:T(8,128)} copy(f32[16,512]{1,0:T(8,128)} %get-tuple-element.16) | data formatting | bytes 65536
  45.1 1.3 %copy.17 = f32[16,256]{1,0:T(8,128)} copy(f32[16,256]{1,0:T(8,128)} %get-tuple-element.17) | data formatting | bytes 32768
  46.5 1.2 %copy.18 = f32[512]{0:T(512)} copy(f32[512]{0:T(512)} %bitcast.6) | data formatting | bytes 4096

commit v2 on v1

v2 whole, which is shorter than its diff:
```python
import functools
import math

import jax
import jax.numpy as jnp
from jax import lax
from jax.experimental import pallas as pl
from jax.experimental.pallas import tpu as pltpu
from jax.sharding import PartitionSpec as P

MESH = pl.DeviceIdType.MESH
F32 = jnp.float32
BF16 = jnp.bfloat16
SIDE = 4
CHIPS = SIDE * SIDE
XS = 4
STEPS = sorted(
    ((a, b) for a in range(SIDE) for b in range(SIDE)),
    key=lambda s: -sum(min(k, SIDE - k) for k in s),
)
HERE = CHIPS - 1
EARLY = 10
NT = (((1,), (1,)), ((), ()))
TN = (((0,), (0,)), ((), ()))
NN = (((1,), (0,)), ((), ()))


def div(a, b):
    return lax.div(a, jnp.int32(b))


def rem(a, b):
    return lax.rem(a, jnp.int32(b))


def div(a, b):
    return lax.div(a, jnp.int32(b))


def rem(a, b):
    return lax.rem(a, jnp.int32(b))


def dot(a, b, dims):
    return lax.dot_general(a, b, dims, preferred_element_type=F32)


def halves(x):
    high = x.astype(BF16)
    return high, (x - high.astype(F32)).astype(BF16)


def kernel(
    norm, geno_hbm, labels_hbm, coef_hbm, index_hbm, count_ref, load_hbm, icpt_hbm,
    gv_ref, gt_ref, score_ref, top_ref,
    geno, labels, coef, index, load, icpt,
    pair_out, pair_in, own, pred_out, pred_in, w_same, w_pair, vp, tops,
    tr_own, tr_core, tr_x, tr_y, tr_z,
    geno_sem, small_sem, pair_send, pair_recv, pred_send, pred_recv,
    w_send, w_recv, relay_send, relay_recv, vp_send, vp_recv, top_send, top_recv,
    tr_send, tr_core_recv, tr_x_recv, tr_y_recv, tr_z_recv,
):
    me = lax.axis_index("var")
    samp = lax.axis_index("samp")
    core = rem(me, 2)
    chip = div(me, 2)
    y, z = div(chip, SIDE), rem(chip, SIDE)
    other = 1 - core
    partner = chip * 2 + other
    ys = [rem(y + k, SIDE) * SIDE for k in range(SIDE)]
    zs = [rem(z + k, SIDE) for k in range(SIDE)]
    xs = [rem(samp + k, XS) for k in range(XS)]
    to_chip = [(ys[a] + zs[b]) * 2 for a, b in STEPS]
    from_chip = [(ys[-a % SIDE] + zs[-b % SIDE]) * 2 for a, b in STEPS]

    def send(src, dst, send_sem, recv_sem, var, samp_at):
        return pltpu.make_async_remote_copy(
            src_ref=src,
            dst_ref=dst,
            send_sem=send_sem,
            recv_sem=recv_sem,
            device_id=(var, samp_at),
            device_id_type=MESH,
        )

    rows = labels.shape[0]

    def geno_copy(i, which):
        at = to_chip[i] + which
        return pltpu.make_async_copy(
            geno_hbm.at[pl.ds(pl.multiple_of(at * rows, rows), rows)], geno.at[at], geno_sem.at[at]
        )

    small = [
        pltpu.make_async_copy(src, dst, small_sem.at[k])
        for k, (src, dst) in enumerate(
            (
                (index_hbm, index),
                (coef_hbm, coef),
                (load_hbm, load),
                (icpt_hbm, icpt),
                (labels_hbm, labels),
            )
        )
    ]
    for copy in small[:2]:
        copy.start()
    for i in range(2):
        geno_copy(i, other).start()
    barrier = pltpu.get_barrier_semaphore()

    def greet(var, samp_at):
        pl.semaphore_signal(barrier, inc=1, device_id=(var, samp_at), device_id_type=MESH)

    for i in range(HERE):
        for which in range(2):
            greet(to_chip[i] + which, samp)
    for step in range(1, XS):
        greet(me, xs[step])
    greet(partner, samp)
    for i in range(2, CHIPS):
        geno_copy(i, other).start()
    for i in range(CHIPS):
        geno_copy(i, core).start()
    for copy in small[2:]:
        copy.start()

    for copy in small[:2]:
        copy.wait()
    slots = index.shape[1]
    width = geno.shape[2]
    live = lax.broadcasted_iota(jnp.int32, (1, slots), 1) < count_ref[0]
    variant = lax.broadcasted_iota(jnp.int32, (width, slots), 0)
    chosen = jnp.where((variant == index[...]) & live, F32(1.0), F32(0.0)).astype(BF16)
    dense = dot(coef[...], chosen, NT).astype(BF16)
    active = dot(jnp.where(live, F32(1.0), F32(0.0)).astype(BF16), chosen, NT)

    def partial(i, which):
        geno_copy(i, which).wait()
        return dot(dense, geno[to_chip[i] + which], NT)

    for i in range(CHIPS):
        pair_out[i] = partial(i, other).astype(BF16)
    pl.semaphore_wait(barrier, 2 * HERE + XS)

    half = CHIPS // 2
    to_pair = [
        send(
            pair_out.at[pl.ds(k * half, half)],
            pair_in.at[pl.ds(k * half, half)],
            pair_send.at[k],
            pair_recv.at[k],
            partner,
            samp,
        )
        for k in range(2)
    ]
    for copy in to_pair:
        copy.start()

    pred = [
        send(
            pred_out.at[i], pred_in.at[i], pred_send.at[i], pred_recv.at[i], to_chip[i] + core, samp
        )
        for i in range(HERE)
    ]

    def send_pred(i, part):
        pred_out[i] = (part + pair_in[i].astype(F32)).astype(BF16)
        pred[i].start()

    for i in range(EARLY):
        own[i] = partial(i, core)
    to_pair[0].wait_recv()
    for i in range(half):
        send_pred(i, own[i])
    to_pair[1].wait_recv()
    for i in range(half, EARLY):
        send_pred(i, own[i])
    for i in range(EARLY, HERE):
        send_pred(i, partial(i, core))
    mine = partial(HERE, core) + pair_in[HERE].astype(F32)

    for copy in small[2:]:
        copy.wait()
    load_h, load_m = halves(load[...])
    load_both = jnp.concatenate([load_h, load_m], axis=0)
    for i in reversed(range(HERE)):
        pred[i].wait_recv()
        mine = mine + pred_in[i].astype(F32)
    mine_h, mine_m = halves(mine)
    eta = (
        dot(
            jnp.concatenate([mine_h, mine_h, mine_m], axis=0),
            jnp.concatenate([load_h, load_m, load_h], axis=0),
            TN,
        )
        + icpt[...]
    )
    resid = 1.0 / (1.0 + jnp.exp(-eta)) - labels[...].astype(F32)
    resid_h, resid_m = halves(resid)
    first = dot(load_both, resid_h, NT)
    rank = load.shape[0]
    weights = first[:rank] + first[rank:] + dot(load_h, resid_m, NT)
    w_same[HERE] = weights.astype(BF16)

    to_same = [
        send(
            w_same.at[HERE], w_same.at[i], w_send.at[i], w_recv.at[i], to_chip[i] + core, samp
        )
        for i in range(HERE)
    ]
    relay = [
        send(w_same.at[i], w_pair.at[i], relay_send.at[i], relay_recv.at[i], partner, samp)
        for i in range(CHIPS)
    ]
    for copy in to_same:
        copy.start()
    relay[HERE].start()

    both = dot(jnp.concatenate([mine_h, mine_m], axis=0), resid_h, NN)
    tr_own[...] = (both[:rank] + both[rank:] + dot(mine_h, resid_m, NN)) * norm
    tr_core_copy = send(tr_own, tr_core, tr_send.at[0], tr_core_recv, partner, samp)
    tr_core_copy.start()

    def same_block(i, total):
        return total + dot(w_same[i], geno[from_chip[i] + core], NN)

    def pair_block(i, total):
        relay[i].wait_recv()
        return total + dot(w_pair[i], geno[from_chip[i] + other], NN)

    def arrived(i):
        to_same[i].wait_recv()
        relay[i].start()

    def ring_copies(slots, at, base, recv_sems, peers):
        return [
            send(
                slots.at[at], slots.at[at], tr_send.at[base + k], recv_sems.at[at], *peer
            )
            for k, peer in enumerate(peers)
        ]

    def ring_start(value, slots, at, base, recv_sems, peers):
        slots[at] = value
        copies = ring_copies(slots, at, base, recv_sems, peers)
        for copy in copies:
            copy.start()
        return copies

    def ring_sum(slots, sources, recv_sems, peer):
        for source in sources:
            send(
                slots.at[source], slots.at[source], tr_send.at[0], recv_sems.at[source], *peer
            ).wait_recv()
        return (slots[0] + slots[1]) + (slots[2] + slots[3])

    x_peers = [(me, xs[k]) for k in range(1, XS)]
    y_peers = [((ys[k] + z) * 2 + core, samp) for k in range(1, SIDE)]
    z_peers = [((y * SIDE + zs[k]) * 2 + core, samp) for k in range(1, SIDE)]
    y_at = [rem(y + k, SIDE) for k in range(1, SIDE)]

    total = same_block(HERE, jnp.zeros((rank, width), F32))
    for i in range(HERE - 1, 10, -1):
        arrived(i)
        total = same_block(i, total)
        total = pair_block(i + 1, total)
    tr_core_copy.wait_recv()
    x_copies = ring_start(tr_own[...] + tr_core[...], tr_x, samp, 1, tr_x_recv, x_peers)
    for i in range(10, 4, -1):
        arrived(i)
        total = same_block(i, total)
        total = pair_block(i + 1, total)
    for i in range(4, -1, -1):
        arrived(i)
        total = same_block(i, total)
    x_total = ring_sum(tr_x, xs[1:], tr_x_recv, x_peers[0])
    y_copies = ring_start(x_total, tr_y, y, 4, tr_y_recv, y_peers)
    for i in range(5, -1, -1):
        total = pair_block(i, total)

    vp[samp] = total.astype(BF16)
    to_x = [
        send(vp.at[samp], vp.at[samp], vp_send.at[k], vp_recv.at[samp], *peer)
        for k, peer in enumerate(x_peers)
    ]
    for copy in to_x:
        copy.start()
    y_total = ring_sum(tr_y, y_at, tr_y_recv, y_peers[0])
    z_copies = ring_start(y_total, tr_z, z, 7, tr_z_recv, z_peers)
    for source in xs[1:]:
        send(
            vp.at[source], vp.at[source], vp_send.at[0], vp_recv.at[source], *x_peers[0]
        ).wait_recv()
    grad = vp[0].astype(F32)
    for source in range(1, XS):
        grad = grad + vp[source].astype(F32)
    grad = grad * norm
    score = jnp.sqrt(jnp.sum(grad * grad, axis=0, keepdims=True))
    score = jnp.where(active > 0.0, F32(0.0), score)
    best = score[:, :128]
    for at in range(128, width, 128):
        best = jnp.maximum(best, score[:, at : at + 128])
    tops[2 * HERE] = best
    to_top = [
        send(
            tops.at[2 * HERE],
            tops.at[2 * i + k],
            top_send.at[2 * i + k],
            top_recv.at[2 * i + k],
            to_chip[i] + which,
            samp,
        )
        for i in range(CHIPS)
        for k, which in enumerate((core, other))
        if 2 * i + k != 2 * HERE
    ]
    for copy in to_top:
        copy.start()
    gv_ref[...] = grad
    score_ref[...] = score
    gt_ref[...] = ring_sum(tr_z, zs[1:], tr_z_recv, z_peers[0])

    for copy in (
        *to_pair, *pred, *to_same, *relay, tr_core_copy, *x_copies, *y_copies, *z_copies, *to_x, *to_top
    ):
        copy.wait_send()
    for copy in to_top:
        copy.wait_recv()
    top_ref[...] = jnp.broadcast_to(
        jnp.max(jnp.max(tops[...], axis=0), axis=1, keepdims=True), top_ref.shape
    )


def keep(*refs):
    *refs, sems = refs
    half = len(refs) // 2
    copies = [
        pltpu.make_async_copy(source, target, sems.at[k])
        for k, (source, target) in enumerate(zip(refs[:half], refs[half:]))
    ]
    for copy in copies:
        copy.start()
    for copy in copies:
        copy.wait()


def per_device(genotypes, labels, act_coef, act_index, act_count, loadings, intercept):
    sample_rows, width = genotypes.shape
    rows, traits = labels.shape
    rank = loadings.shape[0]
    slots = act_index.shape[0]
    norm = 1.0 / math.sqrt(sample_rows * lax.axis_size("samp"))
    dma = pltpu.SemaphoreType.DMA
    anywhere = pl.BlockSpec(memory_space=pl.ANY)
    vmem = pl.BlockSpec(memory_space=pltpu.VMEM)
    blocks = (CHIPS, rank, rows)
    trait = (rank, traits)
    in_hbm = functools.partial(pltpu.with_memory_space_constraint, memory_space=pltpu.HBM)
    results = pl.pallas_call(
        functools.partial(kernel, norm),
        out_shape=(
            jax.ShapeDtypeStruct((rank, width), F32),
            jax.ShapeDtypeStruct(trait, F32),
            jax.ShapeDtypeStruct((1, width), F32),
            jax.ShapeDtypeStruct((1, 128), F32),
        ),
        in_specs=[
            *(anywhere,) * 4,
            pl.BlockSpec(memory_space=pltpu.SMEM),
            *(anywhere,) * 2,
        ],
        out_specs=(vmem,) * 4,
        scratch_shapes=[
            pltpu.VMEM((2 * CHIPS, rows, width), BF16),
            pltpu.VMEM((rows, traits), jnp.int32),
            pltpu.VMEM((rank, slots), BF16),
            pltpu.VMEM((1, slots), jnp.int32),
            pltpu.VMEM(trait, F32),
            pltpu.VMEM((1, traits), F32),
            pltpu.VMEM(blocks, BF16),
            pltpu.VMEM(blocks, BF16),
            pltpu.VMEM((EARLY, rank, rows), F32),
            pltpu.VMEM(blocks, BF16),
            pltpu.VMEM(blocks, BF16),
            pltpu.VMEM(blocks, BF16),
            pltpu.VMEM(blocks, BF16),
            pltpu.VMEM((XS, rank, width), BF16),
            pltpu.VMEM((2 * CHIPS, 1, 128), F32),
            pltpu.VMEM(trait, F32),
            pltpu.VMEM(trait, F32),
            pltpu.VMEM((XS, *trait), F32),
            pltpu.VMEM((SIDE, *trait), F32),
            pltpu.VMEM((SIDE, *trait), F32),
            dma((2 * CHIPS,)),
            dma((5,)),
            dma((2,)),
            dma((2,)),
            dma((CHIPS,)),
            dma((CHIPS,)),
            dma((CHIPS,)),
            dma((CHIPS,)),
            dma((CHIPS,)),
            dma((CHIPS,)),
            dma((XS,)),
            dma((XS,)),
            dma((2 * CHIPS,)),
            dma((2 * CHIPS,)),
            dma((10,)),
            dma,
            dma((XS,)),
            dma((SIDE,)),
            dma((SIDE,)),
        ],
        compiler_params=pltpu.CompilerParams(
            collective_id=0, has_side_effects=True, vmem_limit_bytes=48 * 1024 * 1024
        ),
    )(
        in_hbm(genotypes),
        in_hbm(labels),
        in_hbm(act_coef),
        in_hbm(act_index.reshape(1, slots)),
        act_count,
        in_hbm(loadings),
        in_hbm(intercept.reshape(1, traits)),
    )
    grad_var, grad_trait, score, top = pl.pallas_call(
        keep,
        out_shape=tuple(jax.ShapeDtypeStruct(x.shape, x.dtype) for x in results),
        in_specs=[anywhere] * len(results),
        out_specs=(anywhere,) * len(results),
        scratch_shapes=[dma((len(results),))],
        compiler_params=pltpu.CompilerParams(vmem_limit_bytes=4 * 1024 * 1024),
    )(*results)
    return grad_var, grad_trait, score.reshape(width), top[0, :1]


def solution(mesh):
    placed = (
        P("samp", "var"),
        P(("samp", "var"), None),
        P(None, "var"),
        P("var"),
        P("var"),
        P(),
        P(),
    )
    return jax.shard_map(
        per_device,
        mesh=mesh,
        in_specs=placed,
        out_specs=(P(None, "var"), P(), P("var"), P()),
        check_vma=False,
    )
```

time: 49.7 us -> 41.7 us (0.84)
  local copies, waits for them, and re-layouts: 3.93 us -> 0 us
  Pallas kernels: 42.5 us -> 40.3 us
  between operations: 3.04 us -> 1.29 us
    unnamed x3 -> x0, local copies, waits for them, and re-layouts: 3.93 us -> none
    pallas_call x1, Pallas kernels: 42.5 us -> 39.6 us  [per_device(): pl.pallas_call(functools.partial(kernel, norm), out_shape=(jax.ShapeDtype...]
    pallas_call x0 -> x1, Pallas kernels: none -> 0.66 us  [per_device(): pl.pallas_call(keep, out_shape=tuple((jax.ShapeDtypeStruct(x.shape, x.dty...]
where the time goes in v2:
time: 41.7 us; the launch traced here: 41.5 us
  Pallas kernels  40.3 us (97%)
  between operations  1.29 us (3%)
    pallas_call x1, Pallas kernels, per_device(): pl.pallas_call(functools.partial(kernel, norm), out_shape=(jax.ShapeDtype...  39.6 us

profile of v2, /device:TPU:1, one launch (start us, length us, event | category | flops | bytes accessed | tf_op | source)
XLA Modules:
  0.0 41.5 jit_solution(4123211369256482648)
XLA Ops:
  1.3 39.6 %shard_map.102 = (f32[16,512]{1,0:T(8,128)S(1)}, f32[16,256]{1,0:T(8,128)S(1)}, f32[1,512]{1,0:T(1,128)S(1)}, f32[1,128]{1,0:T(1,128)S(1)}) custom-call(bf16[12288,512]{1,0:T(8,128)(2,1)} %geno_hbm.1, s32[384,256]{1,0:T(8,128)} %labels_hbm.1, bf16[16,256]{1,0:T(8,128)(2,1)} %coef_hbm.1, s32[1,256]{1,0:T(1,128)} %bitcast.5, s32[1]{0:T(128)S(6)} %copy.11.count_ref, ...), custom_call_target="tpu_custom_call" | custom-call | tf_op jit(solution)/shard_map/pallas_call | solution.py:361
  40.9 0.7 %shard_map.103 = (f32[16,512]{1,0:T(8,128)}, f32[16,256]{1,0:T(8,128)}, f32[1,512]{1,0:T(1,128)}, f32[1,128]{1,0:T(1,128)}) custom-call(f32[16,512]{1,0:T(8,128)S(1)} %get-tuple-element.12.refs_0_, f32[16,256]{1,0:T(8,128)S(1)} %get-tuple-element.13.refs_1_, f32[1,512]{1,0:T(1,128)S(1)} %get-tuple-element.14.refs_2_, f32[1,128]{1,0:T(1,128)S(1)} %get-tuple-element.15.refs_3_), custom_call_target="tpu_custom_call" | custom-call | tf_op jit(solution)/shard_map/pallas_call | solution.py:428

commit v3 on v2

--- a/solution.py
+++ b/solution.py
@@ -19,7 +19,9 @@
     key=lambda s: -sum(min(k, SIDE - k) for k in s),
 )
 HERE = CHIPS - 1
-EARLY = 10
+BATCHES = ((0, 1), (2, 3), (4, 5), (6, 7, 8), (9, 10, 11), (12, 13), (14, 15))
+BEFORE = 3
+NEAR, MIDDLE, FAR = (15, 14, 13, 12, 11), (10, 9, 8, 7, 6, 5), (4, 3, 2, 1)
 NT = (((1,), (1,)), ((), ()))
 TN = (((0,), (0,)), ((), ()))
 NN = (((1,), (0,)), ((), ()))
@@ -54,10 +56,9 @@
     norm, geno_hbm, labels_hbm, coef_hbm, index_hbm, count_ref, load_hbm, icpt_hbm,
     gv_ref, gt_ref, score_ref, top_ref,
     geno, labels, coef, index, load, icpt,
-    pair_out, pair_in, own, pred_out, pred_in, w_same, w_pair, vp, tops,
+    pred_out, pred_in, w_in, vp, tops,
     tr_own, tr_core, tr_x, tr_y, tr_z,
-    geno_sem, small_sem, pair_send, pair_recv, pred_send, pred_recv,
-    w_send, w_recv, relay_send, relay_recv, vp_send, vp_recv, top_send, top_recv,
+    geno_sem, small_sem, pred_send, pred_recv, w_send, w_recv, vp_send, vp_recv, top_send, top_recv,
     tr_send, tr_core_recv, tr_x_recv, tr_y_recv, tr_z_recv,
 ):
     me = lax.axis_index("var")
@@ -70,8 +71,8 @@
     ys = [rem(y + k, SIDE) * SIDE for k in range(SIDE)]
     zs = [rem(z + k, SIDE) for k in range(SIDE)]
     xs = [rem(samp + k, XS) for k in range(XS)]
-    to_chip = [(ys[a] + zs[b]) * 2 for a, b in STEPS]
-    from_chip = [(ys[-a % SIDE] + zs[-b % SIDE]) * 2 for a, b in STEPS]
+    to_chip = [ys[a] + zs[b] for a, b in STEPS]
+    from_chip = [ys[-a % SIDE] + zs[-b % SIDE] for a, b in STEPS]
 
     def send(src, dst, send_sem, recv_sem, var, samp_at):
         return pltpu.make_async_remote_copy(
@@ -85,10 +86,12 @@
 
     rows = labels.shape[0]
 
-    def geno_copy(i, which):
-        at = to_chip[i] + which
+    def geno_copy(i):
+        at = to_chip[i]
         return pltpu.make_async_copy(
-            geno_hbm.at[pl.ds(pl.multiple_of(at * rows, rows), rows)], geno.at[at], geno_sem.at[at]
+            geno_hbm.at[pl.ds(pl.multiple_of(at * 2 * rows, 2 * rows), 2 * rows)],
+            geno.at[at],
+            geno_sem.at[i],
         )
 
     small = [
@@ -106,7 +109,7 @@
     for copy in small[:2]:
         copy.start()
     for i in range(2):
-        geno_copy(i, other).start()
+        geno_copy(i).start()
     barrier = pltpu.get_barrier_semaphore()
 
     def greet(var, samp_at):
@@ -114,14 +117,12 @@
 
     for i in range(HERE):
         for which in range(2):
-            greet(to_chip[i] + which, samp)
+            greet(to_chip[i] * 2 + which, samp)
     for step in range(1, XS):
         greet(me, xs[step])
     greet(partner, samp)
     for i in range(2, CHIPS):
-        geno_copy(i, other).start()
-    for i in range(CHIPS):
-        geno_copy(i, core).start()
+        geno_copy(i).start()
     for copy in small[2:]:
         copy.start()
 
@@ -135,59 +136,64 @@
     dense = dot(coef[...], chosen, NT).astype(BF16)
     active = dot(jnp.where(live, F32(1.0), F32(0.0)).astype(BF16), chosen, NT)
 
-    def partial(i, which):
-        geno_copy(i, which).wait()
-        return dot(dense, geno[to_chip[i] + which], NT)
-
-    for i in range(CHIPS):
-        pair_out[i] = partial(i, other).astype(BF16)
-    pl.semaphore_wait(barrier, 2 * HERE + XS)
-
-    half = CHIPS // 2
-    to_pair = [
+    def across(source, target, send_sem, recv_sem, i, which):
+        return send(
+            source,
+            target.at[2 * i + core],
+            send_sem.at[2 * i + which],
+            recv_sem.at[2 * i + core],
+            to_chip[i] * 2 + which,
+            samp,
+        )
+
+    def landed(target, send_sem, recv_sem, i, which):
         send(
-            pair_out.at[pl.ds(k * half, half)],
-            pair_in.at[pl.ds(k * half, half)],
-            pair_send.at[k],
-            pair_recv.at[k],
+            target.at[2 * i + which],
+            target.at[2 * i + which],
+            send_sem.at[2 * i],
+            recv_sem.at[2 * i + which],
             partner,
             samp,
-        )
-        for k in range(2)
+        ).wait_recv()
+
+    pred = [
+        across(pred_out.at[2 * i + which], pred_in, pred_send, pred_recv, i, which)
+        for i in range(HERE)
+        for which in range(2)
     ]
-    for copy in to_pair:
-        copy.start()
-
-    pred = [
-        send(
-            pred_out.at[i], pred_in.at[i], pred_send.at[i], pred_recv.at[i], to_chip[i] + core, samp
-        )
-        for i in range(HERE)
-    ]
-
-    def send_pred(i, part):
-        pred_out[i] = (part + pair_in[i].astype(F32)).astype(BF16)
-        pred[i].start()
-
-    for i in range(EARLY):
-        own[i] = partial(i, core)
-    to_pair[0].wait_recv()
-    for i in range(half):
-        send_pred(i, own[i])
-    to_pair[1].wait_recv()
-    for i in range(half, EARLY):
-        send_pred(i, own[i])
-    for i in range(EARLY, HERE):
-        send_pred(i, partial(i, core))
-    mine = partial(HERE, core) + pair_in[HERE].astype(F32)
+    pred_pair = across(pred_out.at[2 * HERE], pred_in, pred_send, pred_recv, HERE, other)
+    for n, batch in enumerate(BATCHES):
+        for i in batch:
+            geno_copy(i).wait()
+        parts = [dot(dense, geno[to_chip[i]], NT) for i in batch]
+        for i, part in zip(batch, parts):
+            if i == HERE:
+                mine = jnp.where(core == 0, part[:, :rows], part[:, rows:])
+                pred_out[2 * HERE] = jnp.where(core == 0, part[:, rows:], part[:, :rows]).astype(BF16)
+            else:
+                for which in range(2):
+                    pred_out[2 * i + which] = part[:, which * rows : (which + 1) * rows].astype(BF16)
+        if n == BEFORE - 1:
+            pl.semaphore_wait(barrier, 2 * HERE + XS)
+        ready = [i for k in BATCHES[: n + 1] for i in k] if n == BEFORE - 1 else batch
+        if n >= BEFORE - 1:
+            for i in ready:
+                if i == HERE:
+                    pred_pair.start()
+                else:
+                    pred[2 * i].start()
+                    pred[2 * i + 1].start()
 
     for copy in small[2:]:
         copy.wait()
     load_h, load_m = halves(load[...])
     load_both = jnp.concatenate([load_h, load_m], axis=0)
-    for i in reversed(range(HERE)):
-        pred[i].wait_recv()
-        mine = mine + pred_in[i].astype(F32)
+    for i in range(HERE):
+        for which in range(2):
+            landed(pred_in, pred_send, pred_recv, i, which)
+        mine = mine + (pred_in[2 * i].astype(F32) + pred_in[2 * i + 1].astype(F32))
+    landed(pred_in, pred_send, pred_recv, HERE, other)
+    mine = mine + pred_in[2 * HERE + other].astype(F32)
     mine_h, mine_m = halves(mine)
     eta = (
         dot(
@@ -202,37 +208,29 @@
     first = dot(load_both, resid_h, NT)
     rank = load.shape[0]
     weights = first[:rank] + first[rank:] + dot(load_h, resid_m, NT)
-    w_same[HERE] = weights.astype(BF16)
-
-    to_same = [
-        send(
-            w_same.at[HERE], w_same.at[i], w_send.at[i], w_recv.at[i], to_chip[i] + core, samp
-        )
-        for i in range(HERE)
-    ]
-    relay = [
-        send(w_same.at[i], w_pair.at[i], relay_send.at[i], relay_recv.at[i], partner, samp)
-        for i in range(CHIPS)
-    ]
-    for copy in to_same:
-        copy.start()
-    relay[HERE].start()
+    w_own = w_in.at[2 * HERE + core]
+    w_own[...] = weights.astype(BF16)
+    to_w = [across(w_own, w_in, w_send, w_recv, HERE, other)]
+    for i in reversed(range(HERE)):
+        for which in range(2):
+            to_w.append(across(w_own, w_in, w_send, w_recv, i, which))
+    for copy in to_w:
+        copy.start()
 
     both = dot(jnp.concatenate([mine_h, mine_m], axis=0), resid_h, NN)
     tr_own[...] = (both[:rank] + both[rank:] + dot(mine_h, resid_m, NN)) * norm
     tr_core_copy = send(tr_own, tr_core, tr_send.at[0], tr_core_recv, partner, samp)
     tr_core_copy.start()
 
-    def same_block(i, total):
-        return total + dot(w_same[i], geno[from_chip[i] + core], NN)
-
-    def pair_block(i, total):
-        relay[i].wait_recv()
-        return total + dot(w_pair[i], geno[from_chip[i] + other], NN)
-
-    def arrived(i):
-        to_same[i].wait_recv()
-        relay[i].start()
+    def products(batch, total):
+        for i in batch:
+            for which in (other,) if i == HERE else (0, 1):
+                landed(w_in, w_send, w_recv, i, which)
+        for i in batch:
+            both = jnp.concatenate([w_in[2 * i], w_in[2 * i + 1]], axis=1)
+            part = dot(both, geno[from_chip[i]], NN)
+            total = part if total is None else total + part
+        return total
 
     def ring_copies(slots, at, base, recv_sems, peers):
         return [
@@ -261,24 +259,14 @@
     z_peers = [((y * SIDE + zs[k]) * 2 + core, samp) for k in range(1, SIDE)]
     y_at = [rem(y + k, SIDE) for k in range(1, SIDE)]
 
-    total = same_block(HERE, jnp.zeros((rank, width), F32))
-    for i in range(HERE - 1, 10, -1):
-        arrived(i)
-        total = same_block(i, total)
-        total = pair_block(i + 1, total)
+    total = products(NEAR, None)
     tr_core_copy.wait_recv()
     x_copies = ring_start(tr_own[...] + tr_core[...], tr_x, samp, 1, tr_x_recv, x_peers)
-    for i in range(10, 4, -1):
-        arrived(i)
-        total = same_block(i, total)
-        total = pair_block(i + 1, total)
-    for i in range(4, -1, -1):
-        arrived(i)
-        total = same_block(i, total)
+    total = products(MIDDLE, total)
+    total = products(FAR, total)
     x_total = ring_sum(tr_x, xs[1:], tr_x_recv, x_peers[0])
     y_copies = ring_start(x_total, tr_y, y, 4, tr_y_recv, y_peers)
-    for i in range(5, -1, -1):
-        total = pair_block(i, total)
+    total = products((0,), total)
 
     vp[samp] = total.astype(BF16)
     to_x = [
@@ -309,7 +297,7 @@
             tops.at[2 * i + k],
             top_send.at[2 * i + k],
             top_recv.at[2 * i + k],
-            to_chip[i] + which,
+            to_chip[i] * 2 + which,
             samp,
         )
         for i in range(CHIPS)
@@ -323,7 +311,7 @@
     gt_ref[...] = ring_sum(tr_z, zs[1:], tr_z_recv, z_peers[0])
 
     for copy in (
-        *to_pair, *pred, *to_same, *relay, tr_core_copy, *x_copies, *y_copies, *z_copies, *to_x, *to_top
+        *pred, pred_pair, *to_w, tr_core_copy, *x_copies, *y_copies, *z_copies, *to_x, *to_top
     ):
         copy.wait_send()
     for copy in to_top:
@@ -355,7 +343,7 @@
     dma = pltpu.SemaphoreType.DMA
     anywhere = pl.BlockSpec(memory_space=pl.ANY)
     vmem = pl.BlockSpec(memory_space=pltpu.VMEM)
-    blocks = (CHIPS, rank, rows)
+    blocks = (2 * CHIPS, rank, rows)
     trait = (rank, traits)
     in_hbm = functools.partial(pltpu.with_memory_space_constraint, memory_space=pltpu.HBM)
     results = pl.pallas_call(
@@ -373,16 +361,12 @@
         ],
         out_specs=(vmem,) * 4,
         scratch_shapes=[
-            pltpu.VMEM((2 * CHIPS, rows, width), BF16),
+            pltpu.VMEM((CHIPS, 2 * rows, width), BF16),
             pltpu.VMEM((rows, traits), jnp.int32),
             pltpu.VMEM((rank, slots), BF16),
             pltpu.VMEM((1, slots), jnp.int32),
             pltpu.VMEM(trait, F32),
             pltpu.VMEM((1, traits), F32),
-            pltpu.VMEM(blocks, BF16),
-            pltpu.VMEM(blocks, BF16),
-            pltpu.VMEM((EARLY, rank, rows), F32),
-            pltpu.VMEM(blocks, BF16),
             pltpu.VMEM(blocks, BF16),
             pltpu.VMEM(blocks, BF16),
             pltpu.VMEM(blocks, BF16),
@@ -393,16 +377,12 @@
             pltpu.VMEM((XS, *trait), F32),
             pltpu.VMEM((SIDE, *trait), F32),
             pltpu.VMEM((SIDE, *trait), F32),
-            dma((2 * CHIPS,)),
+            dma((CHIPS,)),
             dma((5,)),
-            dma((2,)),
-            dma((2,)),
-            dma((CHIPS,)),
-            dma((CHIPS,)),
-            dma((CHIPS,)),
-            dma((CHIPS,)),
-            dma((CHIPS,)),
-            dma((CHIPS,)),
+            dma((2 * CHIPS,)),
+            dma((2 * CHIPS,)),
+            dma((2 * CHIPS,)),
+            dma((2 * CHIPS,)),
             dma((XS,)),
             dma((XS,)),
             dma((2 * CHIPS,)),

time: 41.7 us -> 37 us (0.89)
  Pallas kernels: 40.3 us -> 35.6 us
    pallas_call x1, Pallas kernels: 39.6 us -> 34.9 us  [per_device(): pl.pallas_call(functools.partial(kernel, norm), out_shape=(jax.ShapeDtype...]
where the time goes in v3:
time: 37 us; the launch traced here: 36.9 us
  Pallas kernels  35.6 us (96%)
  between operations  1.29 us (3%)
    pallas_call x1, Pallas kernels, per_device(): pl.pallas_call(functools.partial(kernel, norm), out_shape=(jax.ShapeDtype...  34.9 us

profile of v3, /device:TPU:1, one launch (start us, length us, event | category | flops | bytes accessed | tf_op | source)
XLA Modules:
  0.0 36.9 jit_solution(37673296021513606)
XLA Ops:
  1.3 34.9 %shard_map.102 = (f32[16,512]{1,0:T(8,128)S(1)}, f32[16,256]{1,0:T(8,128)S(1)}, f32[1,512]{1,0:T(1,128)S(1)}, f32[1,128]{1,0:T(1,128)S(1)}) custom-call(bf16[12288,512]{1,0:T(8,128)(2,1)} %geno_hbm.1, s32[384,256]{1,0:T(8,128)} %labels_hbm.1, bf16[16,256]{1,0:T(8,128)(2,1)} %coef_hbm.1, s32[1,256]{1,0:T(1,128)} %bitcast.5, s32[1]{0:T(128)S(6)} %copy.11.count_ref, ...), custom_call_target="tpu_custom_call" | custom-call | tf_op jit(solution)/shard_map/pallas_call | solution.py:349
  36.2 0.7 %shard_map.103 = (f32[16,512]{1,0:T(8,128)}, f32[16,256]{1,0:T(8,128)}, f32[1,512]{1,0:T(1,128)}, f32[1,128]{1,0:T(1,128)}) custom-call(f32[16,512]{1,0:T(8,128)S(1)} %get-tuple-element.12.refs_0_, f32[16,256]{1,0:T(8,128)S(1)} %get-tuple-element.13.refs_1_, f32[1,512]{1,0:T(1,128)S(1)} %get-tuple-element.14.refs_2_, f32[1,128]{1,0:T(1,128)S(1)} %get-tuple-element.15.refs_3_), custom_call_target="tpu_custom_call" | custom-call | tf_op jit(solution)/shard_map/pallas_call | solution.py:408

commit v4 on v3

--- a/solution.py
+++ b/solution.py
@@ -21,7 +21,7 @@
 HERE = CHIPS - 1
 BATCHES = ((0, 1), (2, 3), (4, 5), (6, 7, 8), (9, 10, 11), (12, 13), (14, 15))
 BEFORE = 3
-NEAR, MIDDLE, FAR = (15, 14, 13, 12, 11), (10, 9, 8, 7, 6, 5), (4, 3, 2, 1)
+GROUPS = ((15, 14, 13, 12, 11), (10, 9, 8, 7, 6, 5), (4, 3, 2, 1), (0,))
 NT = (((1,), (1,)), ((), ()))
 TN = (((0,), (0,)), ((), ()))
 NN = (((1,), (0,)), ((), ()))
@@ -59,7 +59,7 @@
     pred_out, pred_in, w_in, vp, tops,
     tr_own, tr_core, tr_x, tr_y, tr_z,
     geno_sem, small_sem, pred_send, pred_recv, w_send, w_recv, vp_send, vp_recv, top_send, top_recv,
-    tr_send, tr_core_recv, tr_x_recv, tr_y_recv, tr_z_recv,
+    tr_send, tr_recv,
 ):
     me = lax.axis_index("var")
     samp = lax.axis_index("samp")
@@ -91,7 +91,7 @@
         return pltpu.make_async_copy(
             geno_hbm.at[pl.ds(pl.multiple_of(at * 2 * rows, 2 * rows), 2 * rows)],
             geno.at[at],
-            geno_sem.at[i],
+            geno_sem.at[next(n for n, batch in enumerate(BATCHES) if i in batch)],
         )
 
     small = [
@@ -138,23 +138,11 @@
 
     def across(source, target, send_sem, recv_sem, i, which):
         return send(
-            source,
-            target.at[2 * i + core],
-            send_sem.at[2 * i + which],
-            recv_sem.at[2 * i + core],
-            to_chip[i] * 2 + which,
-            samp,
-        )
-
-    def landed(target, send_sem, recv_sem, i, which):
-        send(
-            target.at[2 * i + which],
-            target.at[2 * i + which],
-            send_sem.at[2 * i],
-            recv_sem.at[2 * i + which],
-            partner,
-            samp,
-        ).wait_recv()
+            source, target.at[2 * i + core], send_sem, recv_sem, to_chip[i] * 2 + which, samp
+        )
+
+    def bytes_of(blocks, sem):
+        return send(blocks, blocks, sem, sem, partner, samp)
 
     pred = [
         across(pred_out.at[2 * i + which], pred_in, pred_send, pred_recv, i, which)
@@ -163,8 +151,8 @@
     ]
     pred_pair = across(pred_out.at[2 * HERE], pred_in, pred_send, pred_recv, HERE, other)
     for n, batch in enumerate(BATCHES):
-        for i in batch:
-            geno_copy(i).wait()
+        whole = geno.at[pl.ds(0, len(batch))]
+        pltpu.make_async_copy(whole, whole, geno_sem.at[n]).wait()
         parts = [dot(dense, geno[to_chip[i]], NT) for i in batch]
         for i, part in zip(batch, parts):
             if i == HERE:
@@ -188,11 +176,9 @@
         copy.wait()
     load_h, load_m = halves(load[...])
     load_both = jnp.concatenate([load_h, load_m], axis=0)
+    bytes_of(pred_in.at[pl.ds(0, 2 * HERE + 1)], pred_recv).wait_recv()
     for i in range(HERE):
-        for which in range(2):
-            landed(pred_in, pred_send, pred_recv, i, which)
         mine = mine + (pred_in[2 * i].astype(F32) + pred_in[2 * i + 1].astype(F32))
-    landed(pred_in, pred_send, pred_recv, HERE, other)
     mine = mine + pred_in[2 * HERE + other].astype(F32)
     mine_h, mine_m = halves(mine)
     eta = (
@@ -210,77 +196,54 @@
     weights = first[:rank] + first[rank:] + dot(load_h, resid_m, NT)
     w_own = w_in.at[2 * HERE + core]
     w_own[...] = weights.astype(BF16)
-    to_w = [across(w_own, w_in, w_send, w_recv, HERE, other)]
+    to_w = [across(w_own, w_in, w_send, w_recv.at[0], HERE, other)]
     for i in reversed(range(HERE)):
         for which in range(2):
-            to_w.append(across(w_own, w_in, w_send, w_recv, i, which))
+            group = next(n for n, batch in enumerate(GROUPS) if i in batch)
+            to_w.append(across(w_own, w_in, w_send, w_recv.at[group], i, which))
     for copy in to_w:
         copy.start()
 
     both = dot(jnp.concatenate([mine_h, mine_m], axis=0), resid_h, NN)
     tr_own[...] = (both[:rank] + both[rank:] + dot(mine_h, resid_m, NN)) * norm
-    tr_core_copy = send(tr_own, tr_core, tr_send.at[0], tr_core_recv, partner, samp)
+    tr_core_copy = send(tr_own, tr_core, tr_send.at[0], tr_recv.at[0], partner, samp)
     tr_core_copy.start()
 
-    def products(batch, total):
-        for i in batch:
-            for which in (other,) if i == HERE else (0, 1):
-                landed(w_in, w_send, w_recv, i, which)
+    def products(group, total):
+        batch = GROUPS[group]
+        arriving = 2 * len(batch) - (1 if HERE in batch else 0)
+        bytes_of(w_in.at[pl.ds(0, arriving)], w_recv.at[group]).wait_recv()
         for i in batch:
             both = jnp.concatenate([w_in[2 * i], w_in[2 * i + 1]], axis=1)
             part = dot(both, geno[from_chip[i]], NN)
             total = part if total is None else total + part
         return total
 
-    def ring_copies(slots, at, base, recv_sems, peers):
-        return [
-            send(
-                slots.at[at], slots.at[at], tr_send.at[base + k], recv_sems.at[at], *peer
-            )
-            for k, peer in enumerate(peers)
-        ]
-
-    def ring_start(value, slots, at, base, recv_sems, peers):
+    def ring_start(value, slots, at, send_sem, recv_sem, peers):
         slots[at] = value
-        copies = ring_copies(slots, at, base, recv_sems, peers)
-        for copy in copies:
-            copy.start()
-        return copies
-
-    def ring_sum(slots, sources, recv_sems, peer):
-        for source in sources:
-            send(
-                slots.at[source], slots.at[source], tr_send.at[0], recv_sems.at[source], *peer
-            ).wait_recv()
+        for peer in peers:
+            send(slots.at[at], slots.at[at], send_sem, recv_sem, *peer).start()
+
+    def ring_sum(slots, recv_sem):
+        bytes_of(slots.at[pl.ds(0, SIDE - 1)], recv_sem).wait_recv()
         return (slots[0] + slots[1]) + (slots[2] + slots[3])
 
     x_peers = [(me, xs[k]) for k in range(1, XS)]
     y_peers = [((ys[k] + z) * 2 + core, samp) for k in range(1, SIDE)]
     z_peers = [((y * SIDE + zs[k]) * 2 + core, samp) for k in range(1, SIDE)]
-    y_at = [rem(y + k, SIDE) for k in range(1, SIDE)]
-
-    total = products(NEAR, None)
+
+    total = products(0, None)
     tr_core_copy.wait_recv()
-    x_copies = ring_start(tr_own[...] + tr_core[...], tr_x, samp, 1, tr_x_recv, x_peers)
-    total = products(MIDDLE, total)
-    total = products(FAR, total)
-    x_total = ring_sum(tr_x, xs[1:], tr_x_recv, x_peers[0])
-    y_copies = ring_start(x_total, tr_y, y, 4, tr_y_recv, y_peers)
-    total = products((0,), total)
+    ring_start(tr_own[...] + tr_core[...], tr_x, samp, tr_send.at[1], tr_recv.at[1], x_peers)
+    for group in range(1, len(GROUPS)):
+        total = products(group, total)
 
     vp[samp] = total.astype(BF16)
-    to_x = [
-        send(vp.at[samp], vp.at[samp], vp_send.at[k], vp_recv.at[samp], *peer)
-        for k, peer in enumerate(x_peers)
-    ]
-    for copy in to_x:
-        copy.start()
-    y_total = ring_sum(tr_y, y_at, tr_y_recv, y_peers[0])
-    z_copies = ring_start(y_total, tr_z, z, 7, tr_z_recv, z_peers)
-    for source in xs[1:]:
-        send(
-            vp.at[source], vp.at[source], vp_send.at[0], vp_recv.at[source], *x_peers[0]
-        ).wait_recv()
+    for peer in x_peers:
+        send(vp.at[samp], vp.at[samp], vp_send, vp_recv, *peer).start()
+    ring_start(ring_sum(tr_x, tr_recv.at[1]), tr_y, y, tr_send.at[2], tr_recv.at[2], y_peers)
+    ring_start(ring_sum(tr_y, tr_recv.at[2]), tr_z, z, tr_send.at[3], tr_recv.at[3], z_peers)
+    bytes_of(vp.at[pl.ds(0, XS - 1)], vp_recv).wait_recv()
     grad = vp[0].astype(F32)
     for source in range(1, XS):
         grad = grad + vp[source].astype(F32)
@@ -290,32 +253,24 @@
     best = score[:, :128]
     for at in range(128, width, 128):
         best = jnp.maximum(best, score[:, at : at + 128])
-    tops[2 * HERE] = best
-    to_top = [
-        send(
-            tops.at[2 * HERE],
-            tops.at[2 * i + k],
-            top_send.at[2 * i + k],
-            top_recv.at[2 * i + k],
-            to_chip[i] * 2 + which,
-            samp,
-        )
-        for i in range(CHIPS)
-        for k, which in enumerate((core, other))
-        if 2 * i + k != 2 * HERE
-    ]
-    for copy in to_top:
-        copy.start()
+    tops[2 * HERE + core] = best
+    top_own = tops.at[2 * HERE + core]
+    for i in range(HERE):
+        for which in range(2):
+            across(top_own, tops, top_send, top_recv, i, which).start()
+    across(top_own, tops, top_send, top_recv, HERE, other).start()
     gv_ref[...] = grad
     score_ref[...] = score
-    gt_ref[...] = ring_sum(tr_z, zs[1:], tr_z_recv, z_peers[0])
-
-    for copy in (
-        *pred, pred_pair, *to_w, tr_core_copy, *x_copies, *y_copies, *z_copies, *to_x, *to_top
-    ):
-        copy.wait_send()
-    for copy in to_top:
-        copy.wait_recv()
+    gt_ref[...] = ring_sum(tr_z, tr_recv.at[3])
+
+    bytes_of(pred_in.at[pl.ds(0, 2 * HERE + 1)], pred_send).wait_send()
+    bytes_of(w_in.at[pl.ds(0, 2 * HERE + 1)], w_send).wait_send()
+    tr_core_copy.wait_send()
+    for k, slots in ((1, tr_x), (2, tr_y), (3, tr_z)):
+        bytes_of(slots.at[pl.ds(0, SIDE - 1)], tr_send.at[k]).wait_send()
+    bytes_of(vp.at[pl.ds(0, XS - 1)], vp_send).wait_send()
+    bytes_of(tops.at[pl.ds(0, 2 * HERE + 1)], top_send).wait_send()
+    bytes_of(tops.at[pl.ds(0, 2 * HERE + 1)], top_recv).wait_recv()
     top_ref[...] = jnp.broadcast_to(
         jnp.max(jnp.max(tops[...], axis=0), axis=1, keepdims=True), top_ref.shape
     )
@@ -377,21 +332,18 @@
             pltpu.VMEM((XS, *trait), F32),
             pltpu.VMEM((SIDE, *trait), F32),
             pltpu.VMEM((SIDE, *trait), F32),
-            dma((CHIPS,)),
+            dma((len(BATCHES),)),
             dma((5,)),
-            dma((2 * CHIPS,)),
-            dma((2 * CHIPS,)),
-            dma((2 * CHIPS,)),
-            dma((2 * CHIPS,)),
-            dma((XS,)),
-            dma((XS,)),
-            dma((2 * CHIPS,)),
-            dma((2 * CHIPS,)),
-            dma((10,)),
-            dma,
-            dma((XS,)),
-            dma((SIDE,)),
-            dma((SIDE,)),
+            dma,
+            dma,
+            dma,
+            dma((len(GROUPS),)),
+            dma,
+            dma,
+            dma,
+            dma,
+            dma((4,)),
+            dma((4,)),
         ],
         compiler_params=pltpu.CompilerParams(
             collective_id=0, has_side_effects=True, vmem_limit_bytes=48 * 1024 * 1024

time: 37 us -> 35 us (0.946)
  Pallas kernels: 35.6 us -> 33.6 us
    pallas_call x1, Pallas kernels: 34.9 us -> 33 us  [per_device(): pl.pallas_call(functools.partial(kernel, norm), out_shape=(jax.ShapeDtype...]
where the time goes in v4:
time: 35 us; the launch traced here: 34.9 us
  Pallas kernels  33.6 us (96%)
  between operations  1.29 us (4%)
    pallas_call x1, Pallas kernels, per_device(): pl.pallas_call(functools.partial(kernel, norm), out_shape=(jax.ShapeDtype...  33 us

profile of v4, /device:TPU:1, one launch (start us, length us, event | category | flops | bytes accessed | tf_op | source)
XLA Modules:
  0.0 34.9 jit_solution(7910208673497219775)
XLA Ops:
  1.3 33.0 %shard_map.102 = (f32[16,512]{1,0:T(8,128)S(1)}, f32[16,256]{1,0:T(8,128)S(1)}, f32[1,512]{1,0:T(1,128)S(1)}, f32[1,128]{1,0:T(1,128)S(1)}) custom-call(bf16[12288,512]{1,0:T(8,128)(2,1)} %geno_hbm.1, s32[384,256]{1,0:T(8,128)} %labels_hbm.1, bf16[16,256]{1,0:T(8,128)(2,1)} %coef_hbm.1, s32[1,256]{1,0:T(1,128)} %bitcast.5, s32[1]{0:T(128)S(6)} %copy.11.count_ref, ...), custom_call_target="tpu_custom_call" | custom-call | tf_op jit(solution)/shard_map/pallas_call | solution.py:304
  34.3 0.7 %shard_map.103 = (f32[16,512]{1,0:T(8,128)}, f32[16,256]{1,0:T(8,128)}, f32[1,512]{1,0:T(1,128)}, f32[1,128]{1,0:T(1,128)}) custom-call(f32[16,512]{1,0:T(8,128)S(1)} %get-tuple-element.12.refs_0_, f32[16,256]{1,0:T(8,128)S(1)} %get-tuple-element.13.refs_1_, f32[1,512]{1,0:T(1,128)S(1)} %get-tuple-element.14.refs_2_, f32[1,128]{1,0:T(1,128)S(1)} %get-tuple-element.15.refs_3_), custom_call_target="tpu_custom_call" | custom-call | tf_op jit(solution)/shard_map/pallas_call | solution.py:360

commit v5 on v4

--- a/solution.py
+++ b/solution.py
@@ -165,12 +165,12 @@
             pl.semaphore_wait(barrier, 2 * HERE + XS)
         ready = [i for k in BATCHES[: n + 1] for i in k] if n == BEFORE - 1 else batch
         if n >= BEFORE - 1:
-            for i in ready:
-                if i == HERE:
-                    pred_pair.start()
-                else:
-                    pred[2 * i].start()
-                    pred[2 * i + 1].start()
+            for which in range(2):
+                for i in ready:
+                    if i != HERE:
+                        pred[2 * i + which].start()
+            if HERE in ready:
+                pred_pair.start()
 
     for copy in small[2:]:
         copy.wait()
@@ -197,10 +197,11 @@
     w_own = w_in.at[2 * HERE + core]
     w_own[...] = weights.astype(BF16)
     to_w = [across(w_own, w_in, w_send, w_recv.at[0], HERE, other)]
-    for i in reversed(range(HERE)):
+    for group, batch in enumerate(GROUPS):
         for which in range(2):
-            group = next(n for n, batch in enumerate(GROUPS) if i in batch)
-            to_w.append(across(w_own, w_in, w_send, w_recv.at[group], i, which))
+            for i in batch:
+                if i != HERE:
+                    to_w.append(across(w_own, w_in, w_send, w_recv.at[group], i, which))
     for copy in to_w:
         copy.start()
 
@@ -228,7 +229,7 @@
         bytes_of(slots.at[pl.ds(0, SIDE - 1)], recv_sem).wait_recv()
         return (slots[0] + slots[1]) + (slots[2] + slots[3])
 
-    x_peers = [(me, xs[k]) for k in range(1, XS)]
+    x_peers = [(me, xs[k]) for k in (2, 1, 3)]
     y_peers = [((ys[k] + z) * 2 + core, samp) for k in range(1, SIDE)]
     z_peers = [((y * SIDE + zs[k]) * 2 + core, samp) for k in range(1, SIDE)]
 
@@ -255,8 +256,8 @@
         best = jnp.maximum(best, score[:, at : at + 128])
     tops[2 * HERE + core] = best
     top_own = tops.at[2 * HERE + core]
-    for i in range(HERE):
-        for which in range(2):
+    for which in range(2):
+        for i in range(HERE):
             across(top_own, tops, top_send, top_recv, i, which).start()
     across(top_own, tops, top_send, top_recv, HERE, other).start()
     gv_ref[...] = grad

time: 35 us -> 34.8 us (level)
  no operation moved by 1% of the time
where the time goes in v5:
time: 34.8 us; the launch traced here: 34.7 us
  Pallas kernels  33.4 us (96%)
  between operations  1.29 us (4%)
    pallas_call x1, Pallas kernels, per_device(): pl.pallas_call(functools.partial(kernel, norm), out_shape=(jax.ShapeDtype...  32.8 us

profile of v5, /device:TPU:1, one launch (start us, length us, event | category | flops | bytes accessed | tf_op | source)
XLA Modules:
  0.0 34.7 jit_solution(14941279749125727687)
XLA Ops:
  1.3 32.8 %shard_map.102 = (f32[16,512]{1,0:T(8,128)S(1)}, f32[16,256]{1,0:T(8,128)S(1)}, f32[1,512]{1,0:T(1,128)S(1)}, f32[1,128]{1,0:T(1,128)S(1)}) custom-call(bf16[12288,512]{1,0:T(8,128)(2,1)} %geno_hbm.1, s32[384,256]{1,0:T(8,128)} %labels_hbm.1, bf16[16,256]{1,0:T(8,128)(2,1)} %coef_hbm.1, s32[1,256]{1,0:T(1,128)} %bitcast.5, s32[1]{0:T(128)S(6)} %copy.11.count_ref, ...), custom_call_target="tpu_custom_call" | custom-call | tf_op jit(solution)/shard_map/pallas_call | solution.py:305
  34.0 0.7 %shard_map.103 = (f32[16,512]{1,0:T(8,128)}, f32[16,256]{1,0:T(8,128)}, f32[1,512]{1,0:T(1,128)}, f32[1,128]{1,0:T(1,128)}) custom-call(f32[16,512]{1,0:T(8,128)S(1)} %get-tuple-element.12.refs_0_, f32[16,256]{1,0:T(8,128)S(1)} %get-tuple-element.13.refs_1_, f32[1,512]{1,0:T(1,128)S(1)} %get-tuple-element.14.refs_2_, f32[1,128]{1,0:T(1,128)S(1)} %get-tuple-element.15.refs_3_), custom_call_target="tpu_custom_call" | custom-call | tf_op jit(solution)/shard_map/pallas_call | solution.py:361
